TPU v7x, 128 devices: a whole 4x4x4 slice. The times are simulated.
128 devices in a mesh: section: 2 (over core), dev: 64 (over x, z, y).
Axes of the slice: x: 4, y: 4, z: 4, core: 2. Of those that a mesh axis runs over, the one named last changes fastest.
Arguments:
- indices: int32 [8192, 32, 8], P(('section', 'dev')), may hold values from 0 to 131071
- pool_len: int32 [32], replicated, may hold values from 1 to 8
- tables: bfloat16 [4194304, 128], P(('section', 'dev')), may hold values from -3 to 3
- w_first: bfloat16 [4096, 4096], P('dev', 'section'), may hold values from -0.09375 to 0.09375
- b_first: bfloat16 [4096], P('section'), may hold values from -3 to 3
- w_out: bfloat16 [4096], P('section'), may hold values from -0.09375 to 0.09375
Outputs:
- logits: float32 [8192], P('dev')
Inputs may be any that keep to these rules, and one draw needn't show every extreme that they name: `indices`: ids of rows of the table named by the second index.
All inputs are finite; a program needn't handle non-finite values.
Results may differ from a plain program's by a relative error of at most 0.0095.
Values may be sent and summed in bfloat16 or wider, within the bound.
No kernel may reach another device: no remote copies, remote signals or barrier semaphores. Data moves between devices by JAX's collectives and lax.ppermute only.
A program may use at most 128 MiB of HBM per device.

v0:
```python
import jax
import jax.numpy as jnp
from jax import lax
from jax.sharding import PartitionSpec as P


def sent_to_all(shard, axis):
    devices = lax.axis_size(axis)
    return lax.all_to_all(
        jnp.broadcast_to(shard[None], (devices, *shard.shape)), axis, 0, 0, tiled=True
    )


def in_order(tiles, dim):
    shape = list(tiles.shape[1:])
    shape[dim] *= tiles.shape[0]
    return jnp.moveaxis(tiles, 0, dim).reshape(shape)


def collect(shard, axis, dim):
    tiles = sent_to_all(shard, axis)
    return in_order(tiles, dim)


def gathered_total(shard, axis):
    return lax.all_gather(shard, axis).sum(0)


def body(indices, pool_len, tables, w_first, b_first, w_out):
    sec_count = lax.axis_size("section")
    dev_count = lax.axis_size("dev")
    devices = sec_count * dev_count
    dev_rows, n_tables, pool_size = indices.shape
    rows_dev, emb_width = tables.shape
    row_split = devices // n_tables
    position = lax.axis_index("section") * dev_count + lax.axis_index("dev")
    table_id = position // row_split
    first_row = position % row_split * rows_dev
    outgoing = jnp.repeat(indices, row_split, axis=1)
    arrived = lax.all_to_all(outgoing, ("section", "dev"), split_axis=1, concat_axis=0, tiled=True)
    all_rows = devices * dev_rows
    wanted = arrived.reshape(all_rows, pool_size) - first_row
    live_slots = jnp.sum(jnp.where(jnp.arange(n_tables) == table_id, pool_len, 0))
    usable = (wanted >= 0) & (wanted < rows_dev) & (jnp.arange(pool_size)[None, :] < live_slots)
    safe_rows = jnp.where(usable, wanted, 0)
    looked = jnp.take(tables, safe_rows, axis=0)
    picked = jnp.where(usable[:, :, None], looked, jnp.zeros((), jnp.bfloat16))
    partial_value = jnp.sum(picked.astype(jnp.float32), axis=1).astype(jnp.bfloat16)
    ordered = jnp.transpose(
        partial_value.reshape(dev_count, sec_count, dev_rows, emb_width), (1, 0, 2, 3)
    )
    received = lax.all_to_all(
        ordered.reshape(devices, dev_rows, emb_width),
        ("section", "dev"),
        split_axis=0,
        concat_axis=0,
        tiled=True,
    )
    summed = jnp.sum(
        received.reshape(n_tables, row_split, dev_rows, emb_width).astype(jnp.float32), axis=1
    )
    features = jnp.transpose(summed.astype(jnp.bfloat16), (1, 0, 2)).reshape(
        dev_rows, n_tables * emb_width
    )
    samples = collect(features, "section", 0)
    whole_weights = lax.all_gather(w_first, "dev", axis=0, tiled=True)
    pre_act = jnp.dot(samples, whole_weights, preferred_element_type=jnp.float32)
    hidden = jnp.maximum(pre_act + b_first.astype(jnp.float32)[None, :], 0.0)
    logit_part = jnp.sum(hidden * w_out.astype(jnp.float32)[None, :], axis=1)
    return gathered_total(logit_part, "section")


def solution(mesh):
    placed = (
        P(("section", "dev"), None, None),
        P(),
        P(("section", "dev"), None),
        P("dev", "section"),
        P("section"),
        P("section"),
    )
    return jax.shard_map(body, mesh=mesh, in_specs=placed, out_specs=P("dev"), check_vma=False)
```

profile of v0, /device:TPU:1, one launch (start us, length us, event | category | flops | bytes accessed | tf_op | source)
XLA Modules:
  0.0 371.7 jit_solution(8074114564195128807)
XLA Ops:
  6.5 0.0 all-gather.4.cloned.1.call-start
  6.5 0.7 all-gather.4.cloned.1.call-update
  7.3 0.9 broadcast_in_dim.42
  8.2 1.0 reshape.131
  9.2 11.5 %all-to-all-start = ((s32[128,1,512]{2,1,0:T(1,128)}), s32[128,1,512]{2,1,0:T(1,128)S(1)}, u32[]{:S(2)}, u32[]{:S(2)}) async-start(s32[128,1,512]{2,1,0:T(1,128)} %reshape.131), calls=%async_computation | async-start | bytes 524288 | tf_op jit(solution)/shard_map/all_to_all | solution.py:40
  20.7 1.3 fusion.5
  22.0 0.6 iota_compare_fusion
  22.7 8.8 %all-to-all-done = s32[128,1,512]{2,1,0:T(1,128)S(1)} async-done(((s32[128,1,512]{2,1,0:T(1,128)}), s32[128,1,512]{2,1,0:T(1,128)S(1)}, u32[]{:S(2)}, u32[]{:S(2)}) %all-to-all-start) | async-done | bytes 262176 | tf_op jit(solution)/shard_map/all_to_all | solution.py:40
  31.5 0.5 broadcast.117
  32.0 1.3 reduce.3
  33.3 0.1 reshape.132
  33.5 0.1 copy.13
  33.6 0.2 sub.42
  33.8 0.2 sub.40
  33.9 0.1 compare_select_fusion
  34.1 2.6 copy.17
  36.6 3.6 reshape.120
  40.3 0.2 and_and_fusion
  40.5 1.7 copy.14
  42.2 1.7 copy.15
  43.9 222.4 %gather_fusion = bf16[65536,128]{1,0:T(8,128)(2,1)} fusion(bf16[32768,128]{1,0:T(8,128)(2,1)} %param.8, s32[65536]{0:T(1024)S(1)} %broadcast_clamp_fusion), kind=kCustom, calls=%fused_computation | custom fusion | bytes 33816576 | tf_op jit(solution)/shard_map/jit(_take)/gather | solution.py:46
  266.3 0.0 copy-start
  266.3 0.0 copy-start.1
  266.3 46.4 %fusion.1 = bf16[8192,128]{1,0:T(8,128)(2,1)S(1)} fusion(bf16[65536,128]{1,0:T(8,128)(2,1)} %gather_fusion, pred[8192,8]{1,0:T(8,128)(4,1)S(1)} %copy.15, pred[8192,8]{1,0:T(8,128)(4,1)S(1)} %copy.14), kind=kLoop, calls=%fused_computation.3 | loop fusion | flops 24117248 | bytes 19005440 | tf_op jit(solution)/shard_map/reduce_sum | solution.py:48
  312.7 1.5 copy.18
  314.2 4.3 %all-to-all-start.1 = ((bf16[128,64,128]{2,1,0:T(8,128)(2,1)}), bf16[128,64,128]{2,1,0:T(8,128)(2,1)S(1)}, u32[]{:S(2)}, u32[]{:S(2)}) async-start(bf16[128,64,128]{2,1,0:T(8,128)(2,1)} %bitcast.41), calls=%async_computation.1 | async-start | bytes 4194304 | tf_op jit(solution)/shard_map/all_to_all | solution.py:52
  318.5 0.0 copy-done
  318.5 0.0 copy-done.1
  318.5 30.1 %all-to-all-done.1 = bf16[128,64,128]{2,1,0:T(8,128)(2,1)S(1)} async-done(((bf16[128,64,128]{2,1,0:T(8,128)(2,1)}), bf16[128,64,128]{2,1,0:T(8,128)(2,1)S(1)}, u32[]{:S(2)}, u32[]{:S(2)}) %all-to-all-start.1) | async-done | bytes 2097184 | tf_op jit(solution)/shard_map/all_to_all | solution.py:52
  348.6 0.4 bitcast_reduce_fusion
  348.9 0.1 copy_bitcast_fusion
  349.0 0.1 broadcast_in_dim.49
  349.1 5.1 %all_to_all.19 = bf16[2,64,4096]{2,1,0:T(8,128)(2,1)S(1)} all-to-all(bf16[2,64,4096]{2,1,0:T(8,128)(2,1)S(1)} %broadcast_in_dim.49), channel_id=1, replica_groups=mesh['section'=2,'dev'=64] {'section'}, dimensions={0} | all-to-all | bytes 2097152 | tf_op jit(solution)/shard_map/all_to_all | solution.py:9
  354.3 0.0 all-gather.4.cloned.1.call-done
  354.3 8.2 %fusion.4 = f32[128]{0:T(128)S(1)} fusion(bf16[128,4096]{1,0:T(8,128)(2,1)S(1)} %bitcast.42, bf16[4096,2048]{1,0:T(8,128)(2,1)} %all-gather.4.cloned.1.call-done, f32[2048]{0:T(1024)S(1)} %convert_element_type.5, f32[2048]{0:T(1024)S(1)} %convert_element_type.4), kind=kOutput, calls=%fused_computation.8 | convolution fusion | flops 2148532224 | bytes 17842688 | tf_op jit(solution)/shard_map/dot_general | solution.py:67
  362.5 1.8 all-gather.1
  364.3 0.5 reduce_sum.55
  (4 shorter events, 0.1 us)
Async XLA Ops:
  6.5 347.7 %all-gather.4.cloned.1.call-start = ((), (), s32[]{:S(2)}) async-start(), calls=%async_computation.3 | async-start | bytes 17039360 | tf_op jit(solution)/shard_map/all_gather | solution.py:66
  9.2 22.3 %all-to-all-start = ((s32[128,1,512]{2,1,0:T(1,128)}), s32[128,1,512]{2,1,0:T(1,128)S(1)}, u32[]{:S(2)}, u32[]{:S(2)}) async-start(s32[128,1,512]{2,1,0:T(1,128)} %reshape.131), calls=%async_computation | async-start | bytes 524288 | tf_op jit(solution)/shard_map/all_to_all | solution.py:40
  266.3 52.2 %copy-start = (bf16[2048]{0:T(1024)(128)(2,1)S(1)}, bf16[2048]{0:T(1024)(128)(2,1)}, u32[]{:S(2)}) copy-start(bf16[2048]{0:T(1024)(128)(2,1)} %param.10) | copy-start | bytes 12292
  266.3 52.2 %copy-start.1 = (bf16[2048]{0:T(1024)(128)(2,1)S(1)}, bf16[2048]{0:T(1024)(128)(2,1)}, u32[]{:S(2)}) copy-start(bf16[2048]{0:T(1024)(128)(2,1)} %param.11) | copy-start | bytes 12292
  314.2 34.4 %all-to-all-start.1 = ((bf16[128,64,128]{2,1,0:T(8,128)(2,1)}), bf16[128,64,128]{2,1,0:T(8,128)(2,1)S(1)}, u32[]{:S(2)}, u32[]{:S(2)}) async-start(bf16[128,64,128]{2,1,0:T(8,128)(2,1)} %bitcast.41), calls=%async_computation.1 | async-start | bytes 4194304 | tf_op jit(solution)/shard_map/all_to_all | solution.py:52
Sparse Core Ops, SparseCore 0:
  10.2 107.0 all-gather.3
where the time goes:
time: 372 us
  local copies, waits for them, and re-layouts  237 us (64%)
  other arithmetic  50.9 us (14%)
  waiting for transfers between devices  39.6 us (11%)
  starting transfers between devices  15.8 us (4%)
  between operations  13.6 us (4%)
  matrix products  8.24 us (2%)
  blocking collectives  6.93 us (2%)
    gather x1, local copies, waits for them, and re-layouts, body(): looked = jnp.take(tables, safe_rows, axis=0)  222 us
    reduce_sum x1, other arithmetic, body(): jnp.sum(picked.astype(jnp.float32), axis=1).astype(jnp.bfloat16)  46.4 us
    all_to_all x1, waiting for transfers between devices, body(): lax.all_to_all(ordered.reshape(devices, dev_rows, emb_width), ('section',...  30.1 us
    all_to_all x1, starting transfers between devices, body(): lax.all_to_all(outgoing, ('section', 'dev'), split_axis=1, concat_axis=0,...  11.5 us
    all_to_all x1, waiting for transfers between devices, body(): lax.all_to_all(outgoing, ('section', 'dev'), split_axis=1, concat_axis=0,...  8.81 us
    dot_general x1, matrix products, body(): jnp.dot(samples, whole_weights, preferred_element_type=jnp.float32)  8.24 us
  transfers between devices with their start and end apart: 3, of which 2 were waited for; matrix products, arithmetic and copies ran while one was open for 77% of the time, Pallas kernels for 0%

commit v1 on v0

--- a/solution.py
+++ b/solution.py
@@ -37,7 +37,10 @@
     table_id = position // row_split
     first_row = position % row_split * rows_dev
     outgoing = jnp.repeat(indices, row_split, axis=1)
-    arrived = lax.all_to_all(outgoing, ("section", "dev"), split_axis=1, concat_axis=0, tiled=True)
+    size = lax.axis_size(("section", "dev"))
+    pieces = jnp.stack(jnp.split(outgoing, size, axis=1), axis=0)
+    pieces = lax.all_to_all(pieces, ("section", "dev"), split_axis=0, concat_axis=0)
+    arrived = jnp.concatenate(pieces, axis=0)
     all_rows = devices * dev_rows
     wanted = arrived.reshape(all_rows, pool_size) - first_row
     live_slots = jnp.sum(jnp.where(jnp.arange(n_tables) == table_id, pool_len, 0))

time: 372 us -> 374 us (level)
  no operation moved by 1% of the time
where the time goes in v1:
time: 374 us
  local copies, waits for them, and re-layouts  237 us (63%)
  other arithmetic  50.9 us (14%)
  waiting for transfers between devices  39.6 us (11%)
  starting transfers between devices  16.6 us (4%)
  between operations  14.6 us (4%)
  matrix products  8.24 us (2%)
  blocking collectives  6.93 us (2%)
    gather x1, local copies, waits for them, and re-layouts, body(): looked = jnp.take(tables, safe_rows, axis=0)  222 us
    reduce_sum x1, other arithmetic, body(): jnp.sum(picked.astype(jnp.float32), axis=1).astype(jnp.bfloat16)  46.4 us
    all_to_all x1, waiting for transfers between devices, body(): lax.all_to_all(ordered.reshape(devices, dev_rows, emb_width), ('section',...  30.1 us
    all_to_all x1, starting transfers between devices, body(): lax.all_to_all(pieces, ('section', 'dev'), split_axis=0, concat_axis=0)  11.5 us
    all_to_all x1, waiting for transfers between devices, body(): lax.all_to_all(pieces, ('section', 'dev'), split_axis=0, concat_axis=0)  8.8 us
    dot_general x1, matrix products, body(): jnp.dot(samples, whole_weights, preferred_element_type=jnp.float32)  8.24 us
  transfers between devices with their start and end apart: 3, of which 2 were waited for; matrix products, arithmetic and copies ran while one was open for 77% of the time, Pallas kernels for 0%

profile of v1, /device:TPU:1, one launch (start us, length us, event | category | flops | bytes accessed | tf_op | source)
XLA Modules:
  0.0 374.0 jit_solution(17397200164476821890)
XLA Ops:
  6.5 0.0 all-gather.4.cloned.1.call-start
  6.5 0.7 all-gather.4.cloned.1.call-update
  7.3 0.9 broadcast_in_dim.42
  9.6 1.0 reshape.125
  10.6 11.5 %all-to-all-start = ((s32[128,1,512]{2,1,0:T(1,128)}), s32[128,1,512]{2,1,0:T(1,128)S(1)}, u32[]{:S(2)}, u32[]{:S(2)}) async-start(s32[128,1,512]{2,1,0:T(1,128)} %reshape.125), calls=%async_computation | async-start | bytes 524288 | tf_op jit(solution)/shard_map/all_to_all | solution.py:42
  22.1 1.3 fusion.5
  23.4 0.7 iota_compare_fusion
  24.1 8.8 %all-to-all-done = s32[128,1,512]{2,1,0:T(1,128)S(1)} async-done(((s32[128,1,512]{2,1,0:T(1,128)}), s32[128,1,512]{2,1,0:T(1,128)S(1)}, u32[]{:S(2)}, u32[]{:S(2)}) %all-to-all-start) | async-done | bytes 262176 | tf_op jit(solution)/shard_map/all_to_all | solution.py:42
  32.9 0.5 broadcast.109
  33.4 1.3 reduce.3
  34.7 0.1 reshape.126
  34.8 0.2 copy.666
  35.1 0.2 copy.667
  35.3 0.2 sub.32
  35.5 0.2 sub.30
  35.7 0.1 compare_select_fusion
  35.8 2.6 copy.671
  38.4 3.6 reshape.114
  42.0 0.2 and_and_fusion
  42.3 1.7 copy.668
  43.9 1.7 copy.669
  45.7 222.0 %gather_fusion = bf16[65536,128]{1,0:T(8,128)(2,1)} fusion(bf16[32768,128]{1,0:T(8,128)(2,1)} %param.8, s32[65536]{0:T(1024)S(1)} %broadcast_clamp_fusion), kind=kCustom, calls=%fused_computation | custom fusion | bytes 33816576 | tf_op jit(solution)/shard_map/jit(_take)/gather | solution.py:49
  267.7 0.0 copy-start
  267.7 0.0 copy-start.1
  267.7 46.4 %fusion.1 = bf16[8192,128]{1,0:T(8,128)(2,1)S(1)} fusion(bf16[65536,128]{1,0:T(8,128)(2,1)} %gather_fusion, pred[8192,8]{1,0:T(8,128)(4,1)S(1)} %copy.669, pred[8192,8]{1,0:T(8,128)(4,1)S(1)} %copy.668), kind=kLoop, calls=%fused_computation.3 | loop fusion | flops 24117248 | bytes 19005440 | tf_op jit(solution)/shard_map/reduce_sum | solution.py:51
  314.1 1.5 copy.672
  315.6 5.1 %all-to-all-start.1 = ((bf16[128,64,128]{2,1,0:T(8,128)(2,1)}), bf16[128,64,128]{2,1,0:T(8,128)(2,1)S(1)}, u32[]{:S(2)}, u32[]{:S(2)}) async-start(bf16[128,64,128]{2,1,0:T(8,128)(2,1)} %bitcast.548), calls=%async_computation.1 | async-start | bytes 4194304 | tf_op jit(solution)/shard_map/all_to_all | solution.py:55
  320.8 0.0 copy-done
  320.8 0.0 copy-done.1
  320.8 30.1 %all-to-all-done.1 = bf16[128,64,128]{2,1,0:T(8,128)(2,1)S(1)} async-done(((bf16[128,64,128]{2,1,0:T(8,128)(2,1)}), bf16[128,64,128]{2,1,0:T(8,128)(2,1)S(1)}, u32[]{:S(2)}, u32[]{:S(2)}) %all-to-all-start.1) | async-done | bytes 2097184 | tf_op jit(solution)/shard_map/all_to_all | solution.py:55
  350.8 0.4 bitcast_reduce_fusion
  351.2 0.1 copy_bitcast_fusion
  351.3 0.1 broadcast_in_dim.49
  351.4 5.1 %all_to_all.15 = bf16[2,64,4096]{2,1,0:T(8,128)(2,1)S(1)} all-to-all(bf16[2,64,4096]{2,1,0:T(8,128)(2,1)S(1)} %broadcast_in_dim.49), channel_id=1, replica_groups=mesh['section'=2,'dev'=64] {'section'}, dimensions={0} | all-to-all | bytes 2097152 | tf_op jit(solution)/shard_map/all_to_all | solution.py:9
  356.5 0.0 all-gather.4.cloned.1.call-done
  356.5 8.2 %fusion.4 = f32[128]{0:T(128)S(1)} fusion(bf16[128,4096]{1,0:T(8,128)(2,1)S(1)} %bitcast.549, bf16[4096,2048]{1,0:T(8,128)(2,1)} %all-gather.4.cloned.1.call-done, f32[2048]{0:T(1024)S(1)} %convert_element_type.5, f32[2048]{0:T(1024)S(1)} %convert_element_type.4), kind=kOutput, calls=%fused_computation.8 | convolution fusion | flops 2148532224 | bytes 17842688 | tf_op jit(solution)/shard_map/dot_general | solution.py:70
  364.8 1.8 all-gather.1
  366.6 0.5 reduce_sum.55
  (132 shorter events, 0.5 us)
Async XLA Ops:
  6.5 350.0 %all-gather.4.cloned.1.call-start = ((), (), s32[]{:S(2)}) async-start(), calls=%async_computation.3 | async-start | bytes 17039360 | tf_op jit(solution)/shard_map/all_gather | solution.py:69
  10.6 22.3 %all-to-all-start = ((s32[128,1,512]{2,1,0:T(1,128)}), s32[128,1,512]{2,1,0:T(1,128)S(1)}, u32[]{:S(2)}, u32[]{:S(2)}) async-start(s32[128,1,512]{2,1,0:T(1,128)} %reshape.125), calls=%async_computation | async-start | bytes 524288 | tf_op jit(solution)/shard_map/all_to_all | solution.py:42
  267.7 53.1 %copy-start = (bf16[2048]{0:T(1024)(128)(2,1)S(1)}, bf16[2048]{0:T(1024)(128)(2,1)}, u32[]{:S(2)}) copy-start(bf16[2048]{0:T(1024)(128)(2,1)} %param.10) | copy-start | bytes 12292
  267.7 53.1 %copy-start.1 = (bf16[2048]{0:T(1024)(128)(2,1)S(1)}, bf16[2048]{0:T(1024)(128)(2,1)}, u32[]{:S(2)}) copy-start(bf16[2048]{0:T(1024)(128)(2,1)} %param.11) | copy-start | bytes 12292
  315.6 35.2 %all-to-all-start.1 = ((bf16[128,64,128]{2,1,0:T(8,128)(2,1)}), bf16[128,64,128]{2,1,0:T(8,128)(2,1)S(1)}, u32[]{:S(2)}, u32[]{:S(2)}) async-start(bf16[128,64,128]{2,1,0:T(8,128)(2,1)} %bitcast.548), calls=%async_computation.1 | async-start | bytes 4194304 | tf_op jit(solution)/shard_map/all_to_all | solution.py:55
Sparse Core Ops, SparseCore 0:
  10.2 107.6 all-gather.3
